TPU v7x, 32 devices: a whole 2x2x4 slice. The times are simulated.
32 devices in a mesh: dp: 4 (over x, core), param: 8 (over z, y).
Axes of the slice: x: 2, y: 2, z: 4, core: 2. Of those that a mesh axis runs over, the one named last changes fastest.
Arguments:
- train_grads: bfloat16 [3584, 212992], P('dp', 'param'), as said below
- query_grads: bfloat16 [128, 212992], P('dp', 'param'), as said below
Outputs:
- scores: float32 [128, 3584], P('param', 'dp')
Inputs may be any that keep to these rules, and one draw needn't show every extreme that they name: `train_grads`: finite real values. `query_grads`: finite real values.
All inputs are finite; a program needn't handle non-finite values.
Results may differ from a plain program's by a relative error of at most 0.0003.
Values may be sent and summed in bfloat16 or wider, within the bound.
A program may use at most 128 MiB of HBM per device.

v0:
```python
import jax
import jax.numpy as jnp
from jax import lax
from jax.sharding import PartitionSpec as P

epsilon = 1e-06


def per_device(train_grads, query_grads):
    queries = lax.all_gather(query_grads, "dp", axis=0, tiled=True)
    products = lax.dot_general(
        queries, train_grads, (((1,), (1,)), ((), ())), preferred_element_type=jnp.float32
    )
    query_norm = jnp.sum(jnp.square(queries.astype(jnp.float32)), axis=1)
    train_norm = jnp.sum(jnp.square(train_grads.astype(jnp.float32)), axis=1)
    products, query_norm = (
        lax.psum_scatter(products, "param", scatter_dimension=0, tiled=True),
        lax.psum_scatter(query_norm, "param", scatter_dimension=0, tiled=True),
    )
    train_norm = lax.psum(train_norm, "param")
    return (
        products
        * lax.rsqrt(query_norm + epsilon)[:, None]
        * lax.rsqrt(train_norm + epsilon)[None, :]
    )


def solution(mesh):
    return jax.shard_map(
        per_device,
        mesh=mesh,
        in_specs=(P("dp", "param"), P("dp", "param")),
        out_specs=P("param", "dp"),
        check_vma=False,
    )
```

profile of v0, /device:TPU:0, one launch (start us, length us, event | category | flops | bytes accessed | tf_op | source)
XLA Modules:
  0.0 154.5 jit_solution(13825321456841834263)
XLA Ops:
  6.5 0.0 all-gather.2.cloned.1.call-start
  6.5 0.7 all-gather.2.cloned.1.call-update
  7.3 0.0 reduce-scatter.2.cloned.1.call-start
  7.3 53.7 %all-gather.2.cloned.1.call-done = bf16[128,26624]{1,0:T(8,128)(2,1)} async-done(((bf16[32,26624]{1,0:T(8,128)(2,1)}), bf16[128,26624]{1,0:T(8,128)(2,1)}) %all-gather.2.cloned.1.call-update) | async-done | bytes 6815760 | tf_op jit(solution)/shard_map/all_gather | solution.py:10
  61.0 22.4 %fusion.1 = f32[128,896]{1,0:T(8,128)} fusion(bf16[128,26624]{1,0:T(8,128)(2,1)} %all-gather.2.cloned.1.call-done, bf16[896,26624]{1,0:T(8,128)(2,1)} %param.2), kind=kOutput, calls=%fused_computation.6 | convolution fusion | flops 6106906624 | bytes 54984704 | tf_op jit(solution)/shard_map/dot_general | solution.py:11
  83.4 0.0 reduce-scatter.2.cloned.1.call-update
  83.5 0.0 copy-start
  83.5 16.4 %multiply_reduce_fusion = f32[896]{0:T(1024)S(1)} fusion(bf16[896,26624]{1,0:T(8,128)(2,1)} %param.2), kind=kLoop, calls=%fused_computation | loop fusion | flops 71564416 | bytes 47713792 | tf_op jit(solution)/shard_map/reduce_sum | solution.py:15
  99.8 0.0 copy-done
  99.8 0.6 dynamic-slice
  101.1 4.4 %multiply_reduce_fusion.1 = f32[128]{0:T(128)S(1)} fusion(bf16[128,26624]{1,0:T(8,128)(2,1)} %all-gather.2.cloned.1.call-done), kind=kLoop, calls=%fused_computation.1 | loop fusion | flops 10223488 | bytes 6816256 | tf_op jit(solution)/shard_map/reduce_sum | solution.py:14
  105.5 21.6 %all-reduce.1 = (f32[896]{0:T(1024)S(1)}, f32[128]{0:T(128)S(1)}) all-reduce(f32[896]{0:T(1024)S(1)} %multiply_reduce_fusion, f32[128]{0:T(128)S(1)} %multiply_reduce_fusion.1), channel_id=1, replica_groups=mesh['dp'=4,'param'=8] {'param'}, use_global_device_ids=true, to_apply=%region_4.0 | all-reduce | flops 1024 | bytes 8192 | tf_op jit(solution)/shard_map/psum | solution.py:20
  127.1 0.1 fusion
  127.1 19.0 %reduce-scatter.2.cloned.1.call-done = f32[16,896]{1,0:T(8,128)} async-done(((f32[128,896]{1,0:T(8,128)}), f32[16,896]{1,0:T(8,128)}) %reduce-scatter.2.cloned.1.call-update) | async-done | bytes 57360 | tf_op jit(solution)/shard_map/reduce_scatter | solution.py:17
  146.2 1.5 multiply_multiply_fusion
  (1 shorter events, 0.0 us)
Async XLA Ops:
  6.5 54.4 %all-gather.2.cloned.1.call-start = ((), (), s32[]{:S(2)}) async-start(), calls=%async_computation.1 | async-start | bytes 8519680 | tf_op jit(solution)/shard_map/all_gather | solution.py:10
  7.3 138.9 %reduce-scatter.2.cloned.1.call-start = ((), (), s32[]{:S(2)}) async-start(), calls=%async_computation.2 | async-start | bytes 516096 | tf_op jit(solution)/shard_map/reduce_scatter | solution.py:17
  83.5 16.4 %copy-start = (u32[32]{0:T(128)S(1)}, u32[32]{0:T(128)}, u32[]{:S(2)}) copy-start(u32[32]{0:T(128)} %constant.7) | copy-start | bytes 388
Sparse Core Ops, SparseCore 0:
  8.9 52.0 all-gather.1
  83.6 62.5 reduce-scatter.1
where the time goes:
time: 155 us
  waiting for transfers between devices  73.4 us (47%)
  matrix products  22.4 us (14%)
  other arithmetic  22.4 us (14%)
  blocking collectives  21.6 us (14%)
  between operations  14.1 us (9%)
    all_gather x1, waiting for transfers between devices, per_device(): queries = lax.all_gather(query_grads, 'dp', axis=0, tiled=True)  53.7 us
    dot_general x1, matrix products, per_device(): lax.dot_general(queries, train_grads, (((1,), (1,)), ((), ())), preferred...  22.4 us
    psum x1, blocking collectives, per_device(): train_norm = lax.psum(train_norm, 'param')  21.6 us
    reduce_scatter x1, waiting for transfers between devices, per_device(): lax.psum_scatter(products, 'param', scatter_dimension=0, tiled=True)  19 us
    reduce_sum x1, other arithmetic, per_device(): train_norm = jnp.sum(jnp.square(train_grads.astype(jnp.float32)), axis=1)  16.4 us
    reduce_sum x1, other arithmetic, per_device(): query_norm = jnp.sum(jnp.square(queries.astype(jnp.float32)), axis=1)  4.39 us
  transfers between devices with their start and end apart: 2, of which 2 were waited for; matrix products, arithmetic and copies ran while one was open for 14% of the time, Pallas kernels for 0%

commit v1 on v0

--- a/solution.py
+++ b/solution.py
@@ -6,8 +6,15 @@
 epsilon = 1e-06
 
 
+def swapped_in(array, name, dim):
+    size = lax.axis_size(name)
+    pieces = jnp.stack([array for _ in range(size)])
+    pieces = lax.all_to_all(pieces, name, split_axis=0, concat_axis=0)
+    return jnp.concatenate(pieces, axis=dim)
+
+
 def per_device(train_grads, query_grads):
-    queries = lax.all_gather(query_grads, "dp", axis=0, tiled=True)
+    queries = swapped_in(query_grads, "dp", 0)
     products = lax.dot_general(
         queries, train_grads, (((1,), (1,)), ((), ())), preferred_element_type=jnp.float32
     )

time: 155 us -> 184 us (1.19)
  blocking collectives: 21.6 us -> 103 us
  waiting for transfers between devices: 73.4 us -> 18.8 us
  local copies, waits for them, and re-layouts: 0.59 us -> 2.78 us
    all_to_all x0 -> x1, blocking collectives: none -> 80.6 us  [swapped_in(): pieces = lax.all_to_all(pieces, name, split_axis=0, concat_axis=0)]
    all_gather x1 -> x0, waiting for transfers between devices: 53.7 us -> none  [per_device(): queries = lax.all_gather(query_grads, 'dp', axis=0, tiled=True)]
    another operation x0 -> x1, local copies, waits for them, and re-layouts: none -> 2.11 us  [swapped_in(): pieces = jnp.stack([array for _ in range(size)])]
  transfers between devices with their start and end apart: 2 -> 1, of which waited for: 2 -> 1; matrix products, arithmetic and copies ran while one was open for 14% -> 12% of each run, Pallas kernels for 0% -> 0%
where the time goes in v1:
time: 184 us
  blocking collectives  103 us (56%)
  matrix products  22.4 us (12%)
  other arithmetic  22.4 us (12%)
  waiting for transfers between devices  18.8 us (10%)
  between operations  14.1 us (8%)
  local copies, waits for them, and re-layouts  2.78 us (2%)
    all_to_all x1, blocking collectives, swapped_in(): pieces = lax.all_to_all(pieces, name, split_axis=0, concat_axis=0)  80.6 us
    psum x1, blocking collectives, per_device(): train_norm = lax.psum(train_norm, 'param')  22.6 us
    dot_general x1, matrix products, per_device(): lax.dot_general(queries, train_grads, (((1,), (1,)), ((), ())), preferred...  22.4 us
    reduce_scatter x1, waiting for transfers between devices, per_device(): lax.psum_scatter(products, 'param', scatter_dimension=0, tiled=True)  18.8 us
    reduce_sum x1, other arithmetic, per_device(): train_norm = jnp.sum(jnp.square(train_grads.astype(jnp.float32)), axis=1)  16.4 us
    reduce_sum x1, other arithmetic, per_device(): query_norm = jnp.sum(jnp.square(queries.astype(jnp.float32)), axis=1)  4.45 us
  transfers between devices with their start and end apart: 1, of which 1 were waited for; matrix products, arithmetic and copies ran while one was open for 12% of the time, Pallas kernels for 0%

profile of v1, /device:TPU:0, one launch (start us, length us, event | category | flops | bytes accessed | tf_op | source)
XLA Modules:
  0.0 183.7 jit_solution(11833250753314936203)
XLA Ops:
  6.5 0.0 reduce-scatter.2.cloned.1.call-start
  6.5 2.1 %stack.2 = bf16[4,32,26624]{2,1,0:T(8,128)(2,1)S(1)} broadcast(bf16[32,26624]{1,0:T(8,128)(2,1)} %param.3), dimensions={1,2} | broadcast | bytes 8519680 | tf_op jit(solution)/shard_map/stack | solution.py:11
  8.7 80.6 %all_to_all.5 = bf16[4,32,26624]{2,1,0:T(8,128)(2,1)} all-to-all(bf16[4,32,26624]{2,1,0:T(8,128)(2,1)S(1)} %stack.2), channel_id=1, replica_groups=mesh['dp'=4,'param'=8] {'dp'}, dimensions={0} | all-to-all | bytes 13631488 | tf_op jit(solution)/shard_map/all_to_all | solution.py:12
  89.2 22.4 %fusion.1 = f32[128,896]{1,0:T(8,128)} fusion(bf16[128,26624]{1,0:T(8,128)(2,1)} %bitcast.4, bf16[896,26624]{1,0:T(8,128)(2,1)} %param.2), kind=kOutput, calls=%fused_computation.6 | convolution fusion | flops 6106906624 | bytes 54984704 | tf_op jit(solution)/shard_map/dot_general | solution.py:18
  111.7 0.0 reduce-scatter.2.cloned.1.call-update
  111.7 0.0 copy-start
  111.7 16.4 %multiply_reduce_fusion = f32[896]{0:T(1024)S(1)} fusion(bf16[896,26624]{1,0:T(8,128)(2,1)} %param.2), kind=kLoop, calls=%fused_computation | loop fusion | flops 71564416 | bytes 47713792 | tf_op jit(solution)/shard_map/reduce_sum | solution.py:22
  128.1 0.0 copy-done
  128.1 0.6 dynamic-slice
  129.3 4.4 %multiply_reduce_fusion.1 = f32[4,32]{1,0:T(4,128)S(1)} fusion(bf16[4,32,26624]{2,1,0:T(8,128)(2,1)} %all_to_all.5), kind=kLoop, calls=%fused_computation.1 | loop fusion | flops 10223488 | bytes 6816256 | tf_op jit(solution)/shard_map/reduce_sum | solution.py:21
  133.8 0.1 reduce_sum.21
  133.9 22.6 %all-reduce.1 = (f32[896]{0:T(1024)S(1)}, f32[128]{0:T(128)S(1)}) all-reduce(f32[896]{0:T(1024)S(1)} %multiply_reduce_fusion, f32[128]{0:T(128)S(1)} %reduce_sum.21), channel_id=1, replica_groups=mesh['dp'=4,'param'=8] {'param'}, use_global_device_ids=true, to_apply=%region_4.0 | all-reduce | flops 1024 | bytes 8192 | tf_op jit(solution)/shard_map/psum | solution.py:27
  156.5 0.1 fusion
  156.6 18.8 %reduce-scatter.2.cloned.1.call-done = f32[16,896]{1,0:T(8,128)} async-done(((f32[128,896]{1,0:T(8,128)}), f32[16,896]{1,0:T(8,128)}) %reduce-scatter.2.cloned.1.call-update) | async-done | bytes 57360 | tf_op jit(solution)/shard_map/reduce_scatter | solution.py:24
  175.4 1.5 multiply_multiply_fusion
  (1 shorter events, 0.0 us)
Async XLA Ops:
  6.5 168.8 %reduce-scatter.2.cloned.1.call-start = ((), (), s32[]{:S(2)}) async-start(), calls=%async_computation.2 | async-start | bytes 516096 | tf_op jit(solution)/shard_map/reduce_scatter | solution.py:24
  111.7 16.4 %copy-start = (u32[32]{0:T(128)S(1)}, u32[32]{0:T(128)}, u32[]{:S(2)}) copy-start(u32[32]{0:T(128)} %constant.7) | copy-start | bytes 388
Sparse Core Ops, SparseCore 0:
  111.8 63.4 reduce-scatter.1
